TPU v7x, 512 devices: a whole 4x8x8 slice. The times are simulated.
512 devices in a mesh: op: 32 (over x, y_hi, core), sec: 16 (over z, y_lo).
Axes of the slice: x: 4, y: 8 (y_hi: 4, y_lo: 2; y = y_hi * 2 + y_lo), z: 8, core: 2. Of those that a mesh axis runs over, the one named last changes fastest.
Arguments:
- psi: bfloat16 [32, 512, 512], P('sec', 'op'), may hold values from -6 to 6
- left_ops: bfloat16 [64, 32, 512, 512], P('op', 'sec'), may hold values from -0.25 to 0.25
- right_ops: bfloat16 [64, 32, 512, 512], P('op', 'sec'), may hold values from -0.03125 to 0.03125
- conn: int32 [64, 32], P('op', 'sec'), may hold values from 0 to 31, as said below
- dims: int32 [32], P('sec'), may hold values from 128 to 512
Outputs:
- sigma: bfloat16 [32, 512, 512], P('sec', 'op')
Inputs may be any that keep to these rules, and one draw needn't show every extreme that they name: conn[k, s] lies in the same group of 2 consecutive sectors as s or in the next group, cyclically over the 32 sectors; both occur.
All inputs are finite; a program needn't handle non-finite values.
Results may differ from a plain program's by a relative error of at most 0.0049.
Values may be sent and summed in bfloat16 or wider, within the bound.
No kernel may reach another device: no remote copies, remote signals or barrier semaphores. Data moves between devices by JAX's collectives and lax.ppermute only.
A program may use at most 64 MiB of HBM per device.

v0:
```python
import jax
import jax.numpy as jnp
from jax import lax
from jax.sharding import Mesh
from jax.sharding import PartitionSpec as P

OP = ("op_0", "op_1", "op_2")


def in_blocks(x, dim, count):
    before, after = (x.shape[:dim], x.shape[dim + 1 :])
    return jnp.moveaxis(x.reshape(*before, count, -1, *after), dim, 0)


def sent_and_summed(x, axis, dim):
    tiles = in_blocks(x, dim, lax.axis_size(axis))
    arrived = lax.all_to_all(tiles, axis, split_axis=0, concat_axis=0, tiled=True)
    return arrived.sum(axis=0)


def sum_in_two_steps(x, axes, dim):
    far, near = axes
    tiles = in_blocks(x, dim, lax.axis_size(far))
    nearer = sent_and_summed(tiles, near, dim + 1)
    arrived = lax.all_to_all(nearer, far, split_axis=0, concat_axis=0, tiled=True)
    return arrived.sum(axis=0)


def side_by_side(arrays, axis, dim, along):
    widths = [a.shape[along] for a in arrays]
    both = jnp.concatenate(arrays, axis=along)
    whole = sum_in_two_steps(both, axis, dim)
    return tuple(jnp.split(whole, [sum(widths[:k]) for k in range(1, len(widths))], axis=along))


def from_behind(block, axis, distance):
    devices = range(lax.axis_size(axis))
    route = [((i - distance) % len(devices), i) for i in devices]
    return lax.ppermute(block, axis, route)


def row_mask(dims, row_start, rows, width):
    row_ids = row_start + jnp.arange(rows, dtype=jnp.int32)
    col_ids = jnp.arange(width, dtype=jnp.int32)
    return (row_ids[None, :, None] < dims[:, None, None]) & (
        col_ids[None, None, :] < dims[:, None, None]
    )


def on_device(psi, left_ops, right_ops, conn, dims):
    sdev, rows, width = psi.shape
    row_start = lax.axis_index(OP) * rows
    masked = jnp.where(row_mask(dims, row_start, rows, width), psi, jnp.zeros_like(psi))
    gathered = lax.all_gather(masked, OP, axis=1, tiled=True)
    half = jnp.einsum(
        "ksij,sjm->ksim", left_ops, gathered, preferred_element_type=jnp.float32
    ).astype(jnp.bfloat16)
    term = jnp.einsum("ksim,ksnm->ksin", half, right_ops, preferred_element_type=jnp.float32)
    group = lax.axis_index("sec")
    slot = conn % sdev
    elsewhere = conn // sdev != group
    slots = jnp.arange(sdev, dtype=jnp.int32)
    hits = slot[:, :, None] == slots[None, None, :]
    own_hot = (hits & ~elsewhere[:, :, None]).astype(jnp.float32)
    next_hot = (hits & elsewhere[:, :, None]).astype(jnp.float32)
    own = jnp.einsum("kst,ksin->tin", own_hot, term, precision=lax.Precision.HIGHEST)
    onward = jnp.einsum("kst,ksin->tin", next_hot, term, precision=lax.Precision.HIGHEST)
    own_rows, onward_rows = side_by_side((own, onward), (("op_0", "op_1"), "op_2"), 1, 0)
    summed = own_rows + from_behind(onward_rows, "sec", 1)
    summed = jnp.where(row_mask(dims, row_start, rows, width), summed, jnp.zeros_like(summed))
    return summed.astype(jnp.bfloat16)


def solution(mesh):
    finer = Mesh(mesh.devices.reshape(4, 4, 2, mesh.shape["sec"]), ("op_0", "op_1", "op_2", "sec"))
    in_specs = (
        P("sec", OP, None),
        P(OP, "sec", None, None),
        P(OP, "sec", None, None),
        P(OP, "sec"),
        P("sec"),
    )
    out_specs = P("sec", OP, None)
    return jax.shard_map(
        on_device, mesh=finer, in_specs=in_specs, out_specs=out_specs, check_vma=False
    )
```

profile of v0, /device:TPU:2, one launch (start us, length us, event | category | flops | bytes accessed | tf_op | source)
XLA Modules:
  0.0 198.4 jit_solution(11831326014869320493)
XLA Ops:
  6.5 0.0 all-gather.2.cloned.1.call-start
  6.5 0.9 iota_compare_fusion
  7.4 0.7 broadcast_compare_fusion.2
  8.1 1.4 and_select_fusion.1
  9.6 0.0 all-gather.2.cloned.1.call-update
  9.6 0.7 and_select_fusion.3
  10.3 0.7 fusion.27
  11.0 60.2 %all-gather.2.cloned.1.call-done = bf16[2,512,512]{2,1,0:T(8,128)(2,1)} async-done(((bf16[2,16,512]{2,1,0:T(8,128)(2,1)}), bf16[2,512,512]{2,1,0:T(8,128)(2,1)}) %all-gather.2.cloned.1.call-update) | async-done | bytes 1048592 | tf_op jit(solution)/shard_map/all_gather | solution.py:54
  71.2 0.0 copy-done
  71.2 6.4 %fusion.4 = f32[2,2,512,512]{3,2,1,0:T(8,128)} fusion(bf16[2,2,512,512]{3,2,1,0:T(8,128)(2,1)S(1)} %copy-done, bf16[2,2,512,512]{3,2,1,0:T(8,128)(2,1)} %param.6, bf16[2,512,512]{2,1,0:T(8,128)(2,1)} %all-gather.2.cloned.1.call-done), kind=kOutput, calls=%fused_computation.5 | convolution fusion | flops 2148532224 | bytes 9437184 | tf_op jit(solution)/shard_map/ksim,ksnm->ksin/dot_general | solution.py:58
  77.6 14.6 %fusion.12 = f32[2,512,512]{2,0,1:T(2,128)S(1)} fusion(f32[2,2,512,512]{3,2,1,0:T(8,128)} %fusion.4, pred[2,2]{1,0:T(4,128)(4,1)S(1)} %get-tuple-element.6, s32[2,2]{1,0:T(2,128)S(1)} %and_select_fusion.3), kind=kOutput, calls=%fused_computation.10 | convolution fusion | flops 25165840 | bytes 6291476 | tf_op jit(solution)/shard_map/kst,ksin->tin/dot_general | solution.py:67
  92.2 0.0 copy-done.1
  92.2 9.7 %fusion.9 = f32[2,512,512]{2,0,1:T(2,128)S(1)} fusion(f32[2,2,512,512]{3,2,1,0:T(8,128)S(1)} %copy-done.1, pred[2,2]{1,0:T(4,128)(4,1)S(1)} %get-tuple-element.5, s32[2,2]{1,0:T(2,128)S(1)} %and_select_fusion.3), kind=kOutput, calls=%fused_computation.9 | convolution fusion | flops 25165840 | bytes 6291476 | tf_op jit(solution)/shard_map/kst,ksin->tin/dot_general | solution.py:66
  101.9 1.9 pad_maximum_fusion
  103.8 1.3 copy.20
  105.1 3.6 %copy.21 = f32[2,16,4,16,512]{4,2,3,1,0:T(4,128)S(1)} copy(f32[2,16,4,16,512]{4,3,0,2,1:T(8,128)S(1)} %bitcast.28) | data formatting | bytes 8388608 | tf_op jit(solution)/shard_map/transpose | solution.py:12
  108.7 8.2 %all_to_all.10 = f32[2,16,4,16,512]{4,2,3,1,0:T(4,128)} all-to-all(f32[2,16,4,16,512]{4,2,3,1,0:T(4,128)S(1)} %copy.21), channel_id=1, replica_groups=mesh['op_0'=4,'op_1'=4,'op_2'=2,'sec'=16] {'op_2'}, dimensions={0} | all-to-all | bytes 8388608 | tf_op jit(solution)/shard_map/all_to_all | solution.py:17
  116.8 5.3 %reduce_sum.18 = f32[16,4,16,512]{3,1,2,0:T(4,128)} reduce(f32[2,16,4,16,512]{4,2,3,1,0:T(4,128)} %all_to_all.10, f32[]{:T(128)} %constant.53.clone.1), dimensions={0}, to_apply=%region_0.1 | reduce | flops 524288 | bytes 6291460 | tf_op jit(solution)/shard_map/reduce_sum | solution.py:18
  122.1 58.1 %all_to_all.11 = f32[16,4,16,512]{3,1,2,0:T(4,128)} all-to-all(f32[16,4,16,512]{3,1,2,0:T(4,128)} %reduce_sum.18), channel_id=1, replica_groups=mesh['op_0'=4,'op_1'=4,'op_2'=2,'sec'=16] {'op_0','op_1'}, dimensions={0} | all-to-all | bytes 4194304 | tf_op jit(solution)/shard_map/all_to_all | solution.py:25
  180.3 1.9 reduce_sum.19
  182.2 0.1 fusion.29
  182.3 3.0 %collective-permute-start = (f32[2,16,512]{2,1,0:T(8,128)S(1)}, f32[2,16,512]{2,1,0:T(8,128)S(1)}, u32[]{:S(2)}, u32[]{:S(2)}) collective-permute-start(f32[2,16,512]{2,1,0:T(8,128)S(1)} %copy.30), channel_id=1, source_target_pairs={{15,0},{0,1},{1,2},{2,3},{3,4},{4,5},{5,6},{6,7},{7,8},{8,9},{9,10... | collective-permute-start | bytes 196616 | tf_op jit(solution)/shard_map/ppermute | solution.py:39
  185.3 5.6 %collective-permute-done = f32[2,16,512]{2,1,0:T(8,128)S(1)} collective-permute-done((f32[2,16,512]{2,1,0:T(8,128)S(1)}, f32[2,16,512]{2,1,0:T(8,128)S(1)}, u32[]{:S(2)}, u32[]{:S(2)}) %collective-permute-start) | collective-permute-done | bytes 65568 | tf_op jit(solution)/shard_map/ppermute | solution.py:39
  190.9 0.7 fusion.17
  (4 shorter events, 0.0 us)
Async XLA Ops:
  6.5 64.7 %copy-start = (bf16[2,2,512,512]{3,2,1,0:T(8,128)(2,1)S(1)}, bf16[2,2,512,512]{3,2,1,0:T(8,128)(2,1)}, u32[]{:S(2)}) copy-start(bf16[2,2,512,512]{3,2,1,0:T(8,128)(2,1)} %param.7) | copy-start | bytes 6291460
  6.5 64.7 %all-gather.2.cloned.1.call-start = ((), (), s32[]{:S(2)}) async-start(), calls=%async_computation.2 | async-start | bytes 1081344 | tf_op jit(solution)/shard_map/all_gather | solution.py:54
  77.6 14.6 %copy-start.1 = (f32[2,2,512,512]{3,2,1,0:T(8,128)S(1)}, f32[2,2,512,512]{3,2,1,0:T(8,128)}, u32[]{:S(2)}) copy-start(f32[2,2,512,512]{3,2,1,0:T(8,128)} %fusion.4) | copy-start | bytes 12582916
  182.3 8.6 %collective-permute-start = (f32[2,16,512]{2,1,0:T(8,128)S(1)}, f32[2,16,512]{2,1,0:T(8,128)S(1)}, u32[]{:S(2)}, u32[]{:S(2)}) collective-permute-start(f32[2,16,512]{2,1,0:T(8,128)S(1)} %copy.30), channel_id=1, source_target_pairs={{15,0},{0,1},{1,2},{2,3},{3,4},{4,5},{5,6},{6,7},{7,8},{8,9},{9,10... | collective-permute-start | bytes 196616 | tf_op jit(solution)/shard_map/ppermute | solution.py:39
Sparse Core Ops, SparseCore 0:
  10.6 60.6 all-gather.1
where the time goes:
time: 199 us; the launch traced here: 198 us
  blocking collectives  66.3 us (33%)
  waiting for transfers between devices  65.9 us (33%)
  matrix products  30.6 us (15%)
  other arithmetic  14.2 us (7%)
  between operations  13.5 us (7%)
  local copies, waits for them, and re-layouts  4.98 us (3%)
  starting transfers between devices  3 us (2%)
    all_gather x1, waiting for transfers between devices, on_device(): gathered = lax.all_gather(masked, OP, axis=1, tiled=True)  60.2 us
    all_to_all x1, blocking collectives, sum_in_two_steps(): lax.all_to_all(nearer, far, split_axis=0, concat_axis=0, tiled=True)  58.1 us
    dot_general x1, matrix products, on_device(): jnp.einsum('kst,ksin->tin', next_hot, term, precision=lax.Precision.HIGHEST)  14.6 us
    dot_general x1, matrix products, on_device(): jnp.einsum('kst,ksin->tin', own_hot, term, precision=lax.Precision.HIGHEST)  9.66 us
    all_to_all x1, blocking collectives, sent_and_summed(): lax.all_to_all(tiles, axis, split_axis=0, concat_axis=0, tiled=True)  8.16 us
    dot_general x1, matrix products, on_device(): jnp.einsum('ksim,ksnm->ksin', half, right_ops, preferred_element_type=jnp...  6.38 us
    ppermute x1, waiting for transfers between devices, from_behind(): return lax.ppermute(block, axis, route)  5.62 us
    reduce_sum x1, other arithmetic, sent_and_summed(): return arrived.sum(axis=0)  5.27 us
  transfers between devices with their start and end apart: 2, of which 2 were waited for; matrix products, arithmetic and copies ran while one was open for 1% of the time, Pallas kernels for 0%

commit v1 on v0

--- a/solution.py
+++ b/solution.py
@@ -51,7 +51,9 @@
     sdev, rows, width = psi.shape
     row_start = lax.axis_index(OP) * rows
     masked = jnp.where(row_mask(dims, row_start, rows, width), psi, jnp.zeros_like(psi))
-    gathered = lax.all_gather(masked, OP, axis=1, tiled=True)
+    gathered = jnp.concatenate(
+        lax.all_to_all(jnp.stack([masked] * lax.axis_size(OP)), OP, 0, 0), axis=1
+    )
     half = jnp.einsum(
         "ksij,sjm->ksim", left_ops, gathered, preferred_element_type=jnp.float32
     ).astype(jnp.bfloat16)

time: 199 us -> 167 us (0.84)
  waiting for transfers between devices: 65.9 us -> 38 us
  between operations: 13.5 us -> 0.12 us
  starting transfers between devices: 3 us -> 13.5 us
  local copies, waits for them, and re-layouts: 4.98 us -> 7.73 us
  other arithmetic: 14.2 us -> 11.7 us
    all_gather x1 -> x0, waiting for transfers between devices: 60.2 us -> none  [on_device(): gathered = lax.all_gather(masked, OP, axis=1, tiled=True)]
    all_to_all x0 -> x1, waiting for transfers between devices: none -> 27.3 us  [on_device(): lax.all_to_all(jnp.stack([masked] * lax.axis_size(OP)), OP, 0, 0)]
    all_to_all x0 -> x1, starting transfers between devices: none -> 10.3 us  [on_device(): lax.all_to_all(jnp.stack([masked] * lax.axis_size(OP)), OP, 0, 0)]
    ppermute x1, waiting for transfers between devices: 5.62 us -> 10.7 us  [from_behind(): return lax.ppermute(block, axis, route)]
  transfers between devices with their start and end apart: 2 -> 2, of which waited for: 2 -> 2; matrix products, arithmetic and copies ran while one was open for 1% -> 0% of each run, Pallas kernels for 0% -> 0%
where the time goes in v1:
time: 167 us
  blocking collectives  65.2 us (39%)
  waiting for transfers between devices  38 us (23%)
  matrix products  30.6 us (18%)
  starting transfers between devices  13.5 us (8%)
  other arithmetic  11.7 us (7%)
  local copies, waits for them, and re-layouts  7.73 us (5%)
    all_to_all x1, blocking collectives, sum_in_two_steps(): lax.all_to_all(nearer, far, split_axis=0, concat_axis=0, tiled=True)  56.4 us
    all_to_all x1, waiting for transfers between devices, on_device(): lax.all_to_all(jnp.stack([masked] * lax.axis_size(OP)), OP, 0, 0)  27.3 us
    dot_general x1, matrix products, on_device(): jnp.einsum('kst,ksin->tin', next_hot, term, precision=lax.Precision.HIGHEST)  14.6 us
    ppermute x1, waiting for transfers between devices, from_behind(): return lax.ppermute(block, axis, route)  10.7 us
    all_to_all x1, starting transfers between devices, on_device(): lax.all_to_all(jnp.stack([masked] * lax.axis_size(OP)), OP, 0, 0)  10.3 us
    dot_general x1, matrix products, on_device(): jnp.einsum('kst,ksin->tin', own_hot, term, precision=lax.Precision.HIGHEST)  9.64 us
    all_to_all x1, blocking collectives, sent_and_summed(): lax.all_to_all(tiles, axis, split_axis=0, concat_axis=0, tiled=True)  8.83 us
    dot_general x1, matrix products, on_device(): jnp.einsum('ksim,ksnm->ksin', half, right_ops, preferred_element_type=jnp...  6.38 us
  transfers between devices with their start and end apart: 2, of which 2 were waited for; matrix products, arithmetic and copies ran while one was open for 0% of the time, Pallas kernels for 0%

profile of v1, /device:TPU:2, one launch (start us, length us, event | category | flops | bytes accessed | tf_op | source)
XLA Modules:
  0.0 166.9 jit_solution(16191313170177686752)
XLA Ops:
  0.0 0.0 copy-start
  0.0 0.9 iota_compare_fusion
  0.9 0.7 broadcast_compare_fusion
  1.6 0.9 and_select_fusion.1
  2.5 1.1 stack.2
  3.6 10.3 %all-to-all-start = ((bf16[32,2,16,512]{3,2,1,0:T(8,128)(2,1)}), bf16[32,2,16,512]{3,2,1,0:T(8,128)(2,1)S(1)}, u32[]{:S(2)}, u32[]{:S(2)}) async-start(bf16[32,2,16,512]{3,2,1,0:T(8,128)(2,1)} %stack.2), calls=%async_computation | async-start | bytes 2097152 | tf_op jit(solution)/shard_map/all_to_all | solution.py:55
  13.9 0.0 copy-done.1
  13.9 27.3 %all-to-all-done = bf16[32,2,16,512]{3,2,1,0:T(8,128)(2,1)S(1)} async-done(((bf16[32,2,16,512]{3,2,1,0:T(8,128)(2,1)}), bf16[32,2,16,512]{3,2,1,0:T(8,128)(2,1)S(1)}, u32[]{:S(2)}, u32[]{:S(2)}) %all-to-all-start) | async-done | bytes 1048608 | tf_op jit(solution)/shard_map/all_to_all | solution.py:55
  41.2 1.0 copy.26
  42.3 6.4 %fusion.4 = f32[2,2,512,512]{3,2,1,0:T(8,128)} fusion(bf16[2,2,512,512]{3,2,1,0:T(8,128)(2,1)S(1)} %copy-done, bf16[2,512,512,1]{2,1,0,3:T(8,128)(2,1)} %bitcast.31, bf16[2,2,512,512]{3,2,1,0:T(8,128)(2,1)} %param.6), kind=kOutput, calls=%fused_computation.5 | convolution fusion | flops 2148532224 | bytes 9437184 | tf_op jit(solution)/shard_map/ksim,ksnm->ksin/dot_general | solution.py:60
  48.7 14.6 %fusion.12 = f32[2,512,512]{2,0,1:T(2,128)S(1)} fusion(f32[2,2,512,512]{3,2,1,0:T(8,128)} %fusion.4, pred[2,2]{1,0:T(4,128)(4,1)S(1)} %get-tuple-element.6, s32[2,2]{1,0:T(2,128)S(1)} %and_select_fusion.3), kind=kOutput, calls=%fused_computation.10 | convolution fusion | flops 25165840 | bytes 6291476 | tf_op jit(solution)/shard_map/kst,ksin->tin/dot_general | solution.py:69
  63.2 0.0 copy-done.2
  63.2 9.6 %fusion.9 = f32[2,512,512]{2,0,1:T(2,128)S(1)} fusion(f32[2,2,512,512]{3,2,1,0:T(8,128)S(1)} %copy-done.2, pred[2,2]{1,0:T(4,128)(4,1)S(1)} %get-tuple-element.5, s32[2,2]{1,0:T(2,128)S(1)} %and_select_fusion.3), kind=kOutput, calls=%fused_computation.9 | convolution fusion | flops 25165840 | bytes 6291476 | tf_op jit(solution)/shard_map/kst,ksin->tin/dot_general | solution.py:68
  72.9 1.9 %pad_maximum_fusion = f32[4,512,512]{2,0,1:T(4,128)S(1)} fusion(f32[2,512,512]{2,0,1:T(2,128)S(1)} %fusion.12, f32[2,512,512]{2,0,1:T(2,128)S(1)} %fusion.9), kind=kLoop, calls=%fused_computation | loop fusion | flops 1048576 | bytes 8388608 | tf_op jit(solution)/shard_map/concatenate | solution.py:31
  74.8 1.3 copy.31
  76.1 3.6 %copy.32 = f32[2,16,4,16,512]{4,2,3,1,0:T(4,128)S(1)} copy(f32[2,16,4,16,512]{4,3,0,2,1:T(8,128)S(1)} %bitcast.30) | data formatting | bytes 8388608 | tf_op jit(solution)/shard_map/transpose | solution.py:12
  79.7 8.8 %all_to_all.15 = f32[2,16,4,16,512]{4,2,3,1,0:T(4,128)} all-to-all(f32[2,16,4,16,512]{4,2,3,1,0:T(4,128)S(1)} %copy.32), channel_id=1, replica_groups=mesh['op_0'=4,'op_1'=4,'op_2'=2,'sec'=16] {'op_2'}, dimensions={0} | all-to-all | bytes 8388608 | tf_op jit(solution)/shard_map/all_to_all | solution.py:17
  88.5 5.3 %reduce_sum.18 = f32[16,4,16,512]{3,1,2,0:T(4,128)} reduce(f32[2,16,4,16,512]{4,2,3,1,0:T(4,128)} %all_to_all.15, f32[]{:T(128)} %constant.53.clone.1), dimensions={0}, to_apply=%region_0.1 | reduce | flops 524288 | bytes 6291460 | tf_op jit(solution)/shard_map/reduce_sum | solution.py:18
  93.8 56.4 %all_to_all.16 = f32[16,4,16,512]{3,1,2,0:T(4,128)} all-to-all(f32[16,4,16,512]{3,1,2,0:T(4,128)} %reduce_sum.18), channel_id=1, replica_groups=mesh['op_0'=4,'op_1'=4,'op_2'=2,'sec'=16] {'op_0','op_1'}, dimensions={0} | all-to-all | bytes 4194304 | tf_op jit(solution)/shard_map/all_to_all | solution.py:25
  150.2 1.9 %reduce_sum.19 = f32[4,16,512]{2,0,1:T(4,128)S(1)} reduce(f32[16,4,16,512]{3,1,2,0:T(4,128)} %all_to_all.16, f32[]{:T(128)} %constant.53.clone.1), dimensions={0}, to_apply=%region_1.2 | reduce | flops 491520 | bytes 2228228 | tf_op jit(solution)/shard_map/reduce_sum | solution.py:26
  152.1 3.3 %collective-permute-start = (f32[2,16,512]{2,0,1:T(2,128)S(1)}, f32[2,16,512]{2,0,1:T(2,128)S(1)}, u32[]{:S(2)}, u32[]{:S(2)}) collective-permute-start(f32[2,16,512]{2,0,1:T(2,128)S(1)} %split.9), channel_id=1, source_target_pairs={{15,0},{0,1},{1,2},{2,3},{3,4},{4,5},{5,6},{6,7},{7,8},{8,9},{9,10... | collective-permute-start | bytes 196616 | tf_op jit(solution)/shard_map/ppermute | solution.py:39
  155.4 10.7 %collective-permute-done = f32[2,16,512]{2,0,1:T(2,128)S(1)} collective-permute-done((f32[2,16,512]{2,0,1:T(2,128)S(1)}, f32[2,16,512]{2,0,1:T(2,128)S(1)}, u32[]{:S(2)}, u32[]{:S(2)}) %collective-permute-start) | collective-permute-done | bytes 65568 | tf_op jit(solution)/shard_map/ppermute | solution.py:39
  166.1 0.1 fusion.15
  166.2 0.6 copy.34
  (8 shorter events, 0.1 us)
Async XLA Ops:
  0.0 42.3 %copy-start = (bf16[2,2,512,512]{3,2,1,0:T(8,128)(2,1)S(1)}, bf16[2,2,512,512]{3,2,1,0:T(8,128)(2,1)}, u32[]{:S(2)}) copy-start(bf16[2,2,512,512]{3,2,1,0:T(8,128)(2,1)} %param.7) | copy-start | bytes 6291460
  0.0 13.9 %copy-start.1 = (s32[2,2]{1,0:T(2,128)S(1)}, s32[2,2]{1,0:T(2,128)}, u32[]{:S(2)}) copy-start(s32[2,2]{1,0:T(2,128)} %param.8) | copy-start | bytes 52
  3.6 37.6 %all-to-all-start = ((bf16[32,2,16,512]{3,2,1,0:T(8,128)(2,1)}), bf16[32,2,16,512]{3,2,1,0:T(8,128)(2,1)S(1)}, u32[]{:S(2)}, u32[]{:S(2)}) async-start(bf16[32,2,16,512]{3,2,1,0:T(8,128)(2,1)} %stack.2), calls=%async_computation | async-start | bytes 2097152 | tf_op jit(solution)/shard_map/all_to_all | solution.py:55
  48.7 14.6 %copy-start.2 = (f32[2,2,512,512]{3,2,1,0:T(8,128)S(1)}, f32[2,2,512,512]{3,2,1,0:T(8,128)}, u32[]{:S(2)}) copy-start(f32[2,2,512,512]{3,2,1,0:T(8,128)} %fusion.4) | copy-start | bytes 12582916
  152.1 14.0 %collective-permute-start = (f32[2,16,512]{2,0,1:T(2,128)S(1)}, f32[2,16,512]{2,0,1:T(2,128)S(1)}, u32[]{:S(2)}, u32[]{:S(2)}) collective-permute-start(f32[2,16,512]{2,0,1:T(2,128)S(1)} %split.9), channel_id=1, source_target_pairs={{15,0},{0,1},{1,2},{2,3},{3,4},{4,5},{5,6},{6,7},{7,8},{8,9},{9,10... | collective-permute-start | bytes 196616 | tf_op jit(solution)/shard_map/ppermute | solution.py:39
